TPU v7x, 32 devices: a whole 2x2x4 slice. The times are simulated.
32 devices in a mesh: seq: 8 (over z, x), fsdp: 4 (over y, core).
Axes of the slice: x: 2, y: 2, z: 4, core: 2. Of those that a mesh axis runs over, the one named last changes fastest.
Arguments:
- tokens: bfloat16 [4, 1024, 2048], P('fsdp', 'seq'), may hold values from -6 to 6
- cotangent: bfloat16 [4, 1024, 2048], P('fsdp', 'seq'), may hold values from -6 to 6
- routes: int32 [4, 1024, 8], P('fsdp', 'seq'), may hold values from 0 to 63, all different within a row; in each aligned block of 128 rows (0 to 127, 128 to 255, ..., all dimensions but the last counted through in order) at most 32 rows name the same one
- norm1_gain: bfloat16 [2048], P(('seq', 'fsdp')), may hold values from 0.099609375 to 1.8984375
- query_weight: bfloat16 [2048, 2048], P(('seq', 'fsdp')), may hold values from -0.125 to 0.125
- key_weight: bfloat16 [2048, 2048], P(('seq', 'fsdp')), may hold values from -0.125 to 0.125
- value_weight: bfloat16 [2048, 2048], P(('seq', 'fsdp')), may hold values from -0.125 to 0.125
- output_weight: bfloat16 [2048, 2048], P(('seq', 'fsdp')), may hold values from -2 to 2
- norm2_gain: bfloat16 [2048], P(('seq', 'fsdp')), may hold values from 0.099609375 to 1.8984375
- router_weight: bfloat16 [2048, 64], P(('seq', 'fsdp')), may hold values from -0.125 to 0.125
- expert_gate: bfloat16 [128, 2048, 512], P(('seq', 'fsdp')), may hold values from -0.125 to 0.125
- expert_up: bfloat16 [128, 2048, 512], P(('seq', 'fsdp')), may hold values from -0.125 to 0.125
- expert_down: bfloat16 [128, 512, 2048], P(('seq', 'fsdp')), may hold values from -0.75 to 0.75
Outputs:
- block_out: bfloat16 [4, 1024, 2048], P('fsdp', 'seq')
- input_grad: float32 [4, 1024, 2048], P('fsdp', 'seq')
- norm1_gain_grad: float32 [2048], P(('seq', 'fsdp'))
- query_weight_grad: float32 [2048, 2048], P(('seq', 'fsdp'))
- key_weight_grad: float32 [2048, 2048], P(('seq', 'fsdp'))
- value_weight_grad: float32 [2048, 2048], P(('seq', 'fsdp'))
- output_weight_grad: float32 [2048, 2048], P(('seq', 'fsdp'))
- norm2_gain_grad: float32 [2048], P(('seq', 'fsdp'))
- router_weight_grad: float32 [2048, 64], P(('seq', 'fsdp'))
- expert_gate_grad: float32 [128, 2048, 512], P(('seq', 'fsdp'))
- expert_up_grad: float32 [128, 2048, 512], P(('seq', 'fsdp'))
- expert_down_grad: float32 [128, 512, 2048], P(('seq', 'fsdp'))
Inputs may be any that keep to these rules, and one draw needn't show every extreme that they name: `routes`: each row names 8 different experts. Among the 128 rows of one device (aligned blocks of the flattened sequences) no expert is named more than 32 times, and in every draw some expert is named exactly 32 times in some block; every expert is named somewhere.
All inputs are finite; a program needn't handle non-finite values.
Results may differ from a plain program's by a relative error of at most 0.02.
Values may be sent and summed in bfloat16 or wider, within the bound.
A program may use at most 448 MiB of HBM per device.

v0:
```python
import jax
import jax.numpy as jnp
from jax import lax
from jax.sharding import PartitionSpec as P

H = 16
HD = 128
SPLIT = 2
AXES = ("seq", "fsdp")
epsilon = 1e-06
rope_base = 50000.0
bf16 = jnp.bfloat16
f32 = jnp.float32


def norm_rows(values, scales):
    mean_sq = jnp.mean(values * values, axis=-1, keepdims=True)
    return values * lax.rsqrt(mean_sq + epsilon) * scales


def rope_tables(positions, head_dim):
    half_dim = head_dim // 2
    frequency = rope_base ** (-(2.0 * jnp.arange(half_dim, dtype=f32)) / head_dim)
    angles = positions.astype(f32)[:, None] * frequency[None, :]
    return (jnp.cos(angles), jnp.sin(angles))


def rotate(values, cosine, sine_tab, inverse):
    half_dim = values.shape[-1] // 2
    low_half = values[..., :half_dim]
    high_half = values[..., half_dim:]
    cos_rows = cosine[:, None, :]
    sin_rows = -sine_tab[:, None, :] if inverse else sine_tab[:, None, :]
    return jnp.concatenate(
        [low_half * cos_rows - high_half * sin_rows, high_half * cos_rows + low_half * sin_rows],
        axis=-1,
    )


def route_weights(logits, chosen):
    expo = jnp.exp(logits)
    probability = expo / jnp.sum(expo, axis=-1, keepdims=True)
    experts = jnp.arange(logits.shape[1], dtype=jnp.int32)
    match = (chosen[:, :, None] == experts).astype(f32)
    picked = jnp.sum(match * probability[:, None, :], axis=-1)
    return picked / jnp.sum(picked, axis=-1, keepdims=True)


def mm(left, right):
    return jnp.dot(left, right, preferred_element_type=f32)


def mm_tn(left, right):
    return lax.dot_general(left, right, (((0,), (0,)), ((), ())), preferred_element_type=f32)


def mm_nt(left, right):
    return lax.dot_general(left, right, (((1,), (1,)), ((), ())), preferred_element_type=f32)


def ein(spec, *args):
    return jnp.einsum(spec, *args, preferred_element_type=f32)


def body(
    tokens,
    cotangent,
    routes,
    norm1_gain,
    query_weight,
    key_weight,
    value_weight,
    output_weight,
    norm2_gain,
    router_weight,
    expert_gate,
    expert_up,
    expert_down,
):
    n_seq = lax.axis_size("seq")
    n_fsdp = lax.axis_size("fsdp")
    n_dev = n_seq * n_fsdp
    seq_at = lax.axis_index("seq")
    dev_at = seq_at * n_fsdp + lax.axis_index("fsdp")
    tok_rows, width = (tokens.shape[1], tokens.shape[2])
    length = tok_rows * n_seq
    heads = H // n_seq
    cols = heads * HD
    shard = query_weight.shape[0]
    experts = router_weight.shape[1]
    top_k = routes.shape[2]
    capacity = tok_rows * top_k // experts * 2
    pieces = expert_gate.shape[0]
    n_loc = max(1, pieces // SPLIT)
    per_loc = pieces // n_loc
    first_expert = dev_at * pieces // SPLIT
    x_own = tokens[0]
    cot_own = cotangent[0]
    chosen = routes[0]
    routes_all = lax.all_gather(chosen, AXES, axis=0, tiled=True)
    x_seq = lax.all_gather(x_own, "seq", axis=0, tiled=True)
    small = jnp.concatenate(
        [
            router_weight,
            norm1_gain[:, None],
            norm2_gain[:, None],
            jnp.zeros((shard, 128 - experts - 2), bf16),
        ],
        axis=1,
    )
    blocks = jnp.concatenate(
        [
            query_weight.reshape(shard, n_seq, cols),
            key_weight.reshape(shard, n_seq, cols),
            value_weight.reshape(shard, n_seq, cols),
            jnp.broadcast_to(small[:, None, :], (shard, n_seq, 128)),
        ],
        axis=2,
    ).transpose(1, 0, 2)
    moved = lax.all_to_all(blocks, "seq", split_axis=0, concat_axis=0, tiled=True)
    packed = lax.all_gather(moved, "fsdp", axis=1).reshape(width, 3 * cols + 128)
    w_qkv = packed[:, : 3 * cols]
    router_full = packed[:, 3 * cols : 3 * cols + experts]
    gain_in = packed[:, 3 * cols + experts].astype(f32)
    gain_mid = packed[:, 3 * cols + experts + 1].astype(f32)
    out_full = lax.all_gather(output_weight, AXES, axis=0, tiled=True)
    out_rows = lax.dynamic_slice_in_dim(out_full, seq_at * cols, cols, 0)
    cot_all = lax.all_gather(cot_own, AXES, axis=0, tiled=True)
    cosine, sine_tab = rope_tables(jnp.arange(length, dtype=jnp.int32), HD)
    normed_in = norm_rows(x_seq.astype(f32), gain_in).astype(bf16)
    qkv = mm(normed_in, w_qkv)
    q = rotate(qkv[:, :cols].reshape(length, heads, HD), cosine, sine_tab, False).astype(bf16)
    k = rotate(qkv[:, cols : 2 * cols].reshape(length, heads, HD), cosine, sine_tab, False).astype(
        bf16
    )
    v = qkv[:, 2 * cols :].astype(bf16).reshape(length, heads, HD)
    scale = HD ** (-0.5)
    scores = ein("qhd,khd->hqk", q, k) * scale
    totals = jnp.log(jnp.sum(jnp.exp(scores), axis=-1))
    probs = jnp.exp(scores - totals[..., None])
    attn_heads = ein("hqk,khd->qhd", probs.astype(bf16), v).astype(bf16)
    attn_flat = attn_heads.reshape(length, cols)
    attn_rows = lax.all_to_all(attn_flat, "seq", split_axis=0, concat_axis=1, tiled=True)
    x_own32 = x_own.astype(f32)
    residual = x_own32 + mm(attn_rows, out_full)
    normed_mid = norm_rows(residual, gain_mid).astype(bf16)
    x_all = lax.all_gather(normed_mid, AXES, axis=0, tiled=True)
    logits_all = mm(x_all, router_full)
    w_all = route_weights(logits_all, routes_all)
    local = first_expert + jnp.arange(n_loc, dtype=jnp.int32)
    match = routes_all.reshape(n_dev, tok_rows, top_k)[:, None] == local[None, :, None, None]
    hit = jnp.any(match, axis=-1)
    w_hit = jnp.sum(jnp.where(match, w_all.reshape(n_dev, 1, tok_rows, top_k), 0.0), axis=-1)
    tri = (jnp.arange(tok_rows)[:, None] <= jnp.arange(tok_rows)[None, :]).astype(bf16)
    place = ein("bet,tu->beu", hit.astype(bf16), tri).astype(jnp.int32) - 1
    slots = jnp.arange(capacity, dtype=jnp.int32)
    pick = hit[:, :, None, :] & (place[:, :, None, :] == slots[None, None, :, None])
    one = pick.astype(bf16)
    w_slot = jnp.sum(jnp.where(pick, w_hit[:, :, None, :], 0.0), axis=-1)
    rows_of = lambda a: ein("best,btd->ebsd", one, a.reshape(n_dev, tok_rows, width)).reshape(
        n_loc, n_dev * capacity, width
    )
    rows_in = rows_of(x_all).astype(bf16)
    rows_cot = rows_of(cot_all)
    w_rows = w_slot.transpose(1, 0, 2).reshape(n_loc, n_dev * capacity, 1)
    rows_grad = (w_rows * rows_cot).astype(bf16)
    gate = expert_gate.reshape(n_loc, per_loc, width, -1)
    up = expert_up.reshape(n_loc, per_loc, width, -1)
    down = expert_down.reshape(n_loc, per_loc, -1, width)
    pre_gate = ein("erd,epdf->eprf", rows_in, gate)
    pre_up = ein("erd,epdf->eprf", rows_in, up)
    sig = jax.nn.sigmoid(pre_gate)
    active = pre_gate * sig
    hidden = (active * pre_up).astype(bf16)
    hidden_grad = ein("erd,epfd->eprf", rows_grad, down)
    gate_grad = (hidden_grad * pre_up * sig * (1.0 + pre_gate * (1.0 - sig))).astype(bf16)
    up_grad = (hidden_grad * active).astype(bf16)
    back = ein("eprf,epdf->erd", gate_grad, gate) + ein("eprf,epdf->erd", up_grad, up)
    out = ein("eprf,epfd->erd", hidden, down)
    w_back = jnp.sum(rows_cot * out, axis=-1)
    spread = (
        lambda a: ein("best,ebsd->btd", one, a.astype(bf16).reshape(n_loc, n_dev, capacity, width))
        .astype(bf16)
        .reshape(n_dev * tok_rows, width)
    )
    back_own = lax.psum_scatter(spread(back), AXES, scatter_dimension=0, tiled=True)
    w_tok = jnp.sum(
        jnp.where(pick, w_back.reshape(n_loc, n_dev, capacity).transpose(1, 0, 2)[..., None], 0.0),
        axis=2,
    )
    w_parts = lax.all_to_all(w_tok, AXES, split_axis=0, concat_axis=0, tiled=True)
    w_by_expert = w_parts.reshape(experts, n_dev * n_loc // experts, tok_rows).sum(axis=1)
    own_match = (chosen[:, :, None] == jnp.arange(experts, dtype=jnp.int32)).astype(f32)
    weight_grad = jnp.sum(own_match * w_by_expert.T[:, None, :], axis=-1)
    moe_own = lax.psum_scatter(spread(w_rows * out), AXES, scatter_dimension=0, tiled=True)
    block_out = (residual + moe_own.astype(f32)).astype(bf16)
    down_grad = ein("eprf,erd->epfd", hidden, rows_grad).reshape(expert_down.shape)
    gate_weight_grad = ein("erd,eprf->epdf", rows_in, gate_grad).reshape(expert_gate.shape)
    up_weight_grad = ein("erd,eprf->epdf", rows_in, up_grad).reshape(expert_up.shape)
    logits = mm(normed_mid, router_full)
    _, route_back = jax.vjp(lambda values: route_weights(values, chosen), logits)
    logit_grad = route_back(weight_grad)[0].astype(bf16)
    normed_total = back_own.astype(f32) + mm_nt(logit_grad, router_full)
    logit_all = lax.all_gather(logit_grad, AXES, axis=0, tiled=True)
    x_cols = lax.dynamic_slice_in_dim(x_all, dev_at * shard, shard, 1)
    grad_router = mm_tn(x_cols, logit_all)
    cot32 = cot_own.astype(f32)
    _, norm_back = jax.vjp(norm_rows, residual, gain_mid)
    resid_part, gain_two = norm_back(normed_total)
    resid_grad = cot32 + resid_part
    resid_seq = lax.all_gather(resid_grad.astype(bf16), "seq", axis=0, tiled=True)
    grad_out_rows = mm_tn(attn_flat, resid_seq)
    grad_output = lax.psum_scatter(grad_out_rows, "fsdp", scatter_dimension=0, tiled=True)
    attn_grad = mm_nt(resid_seq, out_rows).astype(bf16).reshape(length, heads, HD)
    delta = jnp.sum(attn_grad.astype(f32) * attn_heads.astype(f32), axis=-1)
    v_grad = ein("hqk,qhd->khd", probs.astype(bf16), attn_grad).astype(bf16)
    p_grad = ein("qhd,khd->hqk", attn_grad, v)
    s_grad = (probs * (p_grad - delta.T[:, :, None]) * scale).astype(bf16)
    q_grad = ein("hqk,khd->qhd", s_grad, k).astype(bf16)
    k_grad = ein("hqk,qhd->khd", s_grad, q).astype(bf16)
    q_rows = rotate(q_grad.astype(f32), cosine, sine_tab, True).astype(bf16)
    k_rows = rotate(k_grad.astype(f32), cosine, sine_tab, True).astype(bf16)
    d_qkv = jnp.concatenate([a.reshape(length, cols) for a in (q_rows, k_rows, v_grad)], axis=1)
    in_part = mm_nt(d_qkv, w_qkv).astype(bf16)
    normed_in_grad = lax.psum_scatter(in_part, "seq", scatter_dimension=0, tiled=True).astype(f32)
    _, norm_back_in = jax.vjp(norm_rows, x_own32, gain_in)
    input_part, gain_one = norm_back_in(normed_in_grad)
    input_grad = resid_grad + input_part
    grad_qkv = mm_tn(normed_in, d_qkv).reshape(n_seq, n_fsdp, shard, 3 * cols)
    grad_qkv = lax.psum_scatter(grad_qkv, "fsdp", scatter_dimension=1, tiled=False)
    grad_qkv = lax.all_to_all(grad_qkv, "seq", split_axis=0, concat_axis=0, tiled=True)
    grad_qkv = (
        grad_qkv.reshape(n_seq, shard, 3, cols).transpose(2, 1, 0, 3).reshape(3, shard, width)
    )
    gains = lax.psum_scatter(
        jnp.stack([gain_one, gain_two]).reshape(2, n_dev, shard),
        AXES,
        scatter_dimension=1,
        tiled=False,
    )
    return (
        block_out[None],
        input_grad[None],
        gains[0],
        grad_qkv[0],
        grad_qkv[1],
        grad_qkv[2],
        grad_output,
        gains[1],
        grad_router,
        gate_weight_grad,
        up_weight_grad,
        down_grad,
    )


def solution(mesh):
    rows3 = P("fsdp", "seq", None)
    flat = P(AXES)
    two = P(AXES, None)
    three = P(AXES, None, None)
    return jax.shard_map(
        body,
        mesh=mesh,
        in_specs=(rows3, rows3, rows3, flat, two, two, two, two, flat, two, three, three, three),
        out_specs=(rows3, rows3, flat, two, two, two, two, flat, two, three, three, three),
        check_vma=False,
    )
```

profile of v0, /device:TPU:0, one launch (start us, length us, event | category | flops | bytes accessed | tf_op | source)
XLA Modules:
  0.0 1324.9 jit_solution(16863959521056442889)
XLA Ops:
  12.9 30.4 %all_to_all.34 = bf16[8,64,896]{2,1,0:T(8,128)(2,1)S(1)} all-to-all(bf16[8,64,896]{2,1,0:T(8,128)(2,1)S(1)} %copy.233), channel_id=1, replica_groups=mesh['seq'=8,'fsdp'=4] {'seq'}, dimensions={0} | all-to-all | bytes 1835008 | tf_op jit(solution)/shard_map/all_to_all | solution.py:120
  46.9 3.1 fusion.80
  50.0 25.2 %all-gather.19.cloned.1.call-done = bf16[8,256,896]{2,0,1:T(8,128)(2,1)} async-done(((bf16[8,64,896]{2,0,1:T(8,128)(2,1)}), bf16[8,256,896]{2,0,1:T(8,128)(2,1)}) %all-gather.19.cloned.1.call-update) | async-done | bytes 3670032 | tf_op jit(solution)/shard_map/all_gather | solution.py:121
  75.1 2.6 copy.235
  77.8 1.8 copy-done.4
  80.2 69.8 %all-gather.17.cloned.1.call-done = bf16[1,1024,2048]{2,1,0:T(8,128)(2,1)} async-done(((bf16[1,128,2048]{2,1,0:T(8,128)(2,1)}), bf16[1,1024,2048]{2,1,0:T(8,128)(2,1)}) %all-gather.17.cloned.1.call-update) | async-done | bytes 4194320 | tf_op jit(solution)/shard_map/all_gather | solution.py:101
  150.0 3.1 fusion.5
  153.7 6.6 fusion.30
  164.2 2.3 fusion.95
  166.5 2.4 copy.296
  168.9 2.4 copy.297
  171.2 3.4 subtract_convert_fusion.3
  174.6 9.4 fusion.8
  184.1 4.2 fusion.36
  189.1 28.2 %all_to_all.35 = bf16[8,128,256]{1,2,0:T(8,128)(2,1)S(1)} all-to-all(bf16[8,128,256]{1,2,0:T(8,128)(2,1)S(1)} %copy.241), channel_id=1, replica_groups=mesh['seq'=8,'fsdp'=4] {'seq'}, dimensions={0} | all-to-all | bytes 1048576 | tf_op jit(solution)/shard_map/all_to_all | solution.py:143
  217.3 14.1 %all-gather.11.cloned.1.call-done = bf16[2048,2048]{1,0:T(8,128)(2,1)} async-done(((bf16[64,2048]{1,0:T(8,128)(2,1)}), bf16[2048,2048]{1,0:T(8,128)(2,1)}) %all-gather.11.cloned.1.call-update) | async-done | bytes 8388624 | tf_op jit(solution)/shard_map/all_gather | solution.py:126
  231.4 4.8 multiply_reduce_fusion.3
  238.2 40.8 %all-gather.2 = s32[1,4096,8]{1,2,0:T(8,128)S(1)} all-gather(s32[1,128,8]{1,2,0:T(8,128)S(1)} %copy-done.24), channel_id=4, replica_groups=mesh['seq'=8,'fsdp'=4] {'seq','fsdp'}, dimensions={1}, use_global_device_ids=true | all-gather | bytes 135168 | tf_op jit(solution)/shard_map/all_gather | solution.py:100
  279.3 68.4 %all-gather.21.cloned.1.call-done = bf16[1,4096,2048]{2,1,0:T(8,128)(2,1)} async-done(((bf16[1,128,2048]{2,1,0:T(8,128)(2,1)}), bf16[1,4096,2048]{2,1,0:T(8,128)(2,1)}) %all-gather.21.cloned.1.call-update) | async-done | bytes 16777232 | tf_op jit(solution)/shard_map/all_gather | solution.py:128
  347.7 7.0 convolution_bitcast_fusion
  354.8 6.2 copy.247
  361.0 102.1 %all-gather.13.cloned.1.call-done = bf16[4096,2048]{1,0:T(8,128)(2,1)} async-done(((bf16[128,2048]{1,0:T(8,128)(2,1)}), bf16[4096,2048]{1,0:T(8,128)(2,1)}) %all-gather.13.cloned.1.call-update) | async-done | bytes 16777232 | tf_op jit(solution)/shard_map/all_gather | solution.py:147
  463.0 9.4 convert_bitcast_fusion
  472.4 8.3 copy.245
  480.7 15.8 %fusion.98 = f32[2,1024,2,512]{3,1,2,0:T(8,128)} fusion(bf16[2,1024,2048,1]{2,1,3,0:T(8,128)(2,1)} %bitcast.248, bf16[2,2,2048,512]{3,2,1,0:T(8,128)(2,1)} %bitcast.297), kind=kOutput, calls=%fused_computation.181 | convolution fusion | flops 8589934592 | bytes 25165824 | tf_op jit(solution)/shard_map/erd,epdf->eprf/dot_general | solution.py:62
  496.4 15.0 %fusion.17 = (bf16[2,2,1024,512]{3,2,1,0:T(8,128)(2,1)S(1)}, f32[2,1024,2,512]{3,1,2,0:T(8,128)}) fusion(f32[2,1024,2,512]{3,1,2,0:T(8,128)} %fusion.98, bf16[2,1024,2048,1]{2,1,3,0:T(8,128)(2,1)S(1)} %bitcast.251, bf16[2,2,2048,512]{3,2,1,0:T(8,128)(2,1)} %bitcast.299), kind=kOutput, calls=%fused_computation.31 | convolution fusion | flops 8602517504 | bytes 37748736 | tf_op jit(solution)/shard_map/erd,epdf->eprf/dot_general | solution.py:62
  511.4 19.9 %fusion.3 = (f32[2,1024]{1,0:T(2,128)S(1)}, f32[2,1024,2048,1]{2,1,3,0:T(8,128)}) fusion(f32[2,32,32,2048]{3,2,1,0:T(8,128)} %copy.247, bf16[2,2,1024,512]{3,2,1,0:T(8,128)(2,1)S(1)} %get-tuple-element.133, bf16[2,2,512,2048]{3,2,1,0:T(8,128)(2,1)} %bitcast.295), kind=kOutput, calls=%fused_computation.8 | convolution fusion | flops 8598321152 | bytes 46145536 | tf_op jit(solution)/shard_map/eprf,epfd->erd/dot_general | solution.py:62
  531.4 11.0 fusion.97
  542.6 1.6 select_reduce_fusion
  545.6 17.0 %fusion.2 = (bf16[2,1024,2048]{2,1,0:T(8,128)(2,1)}, bf16[2,1024,2048]{2,1,0:T(8,128)(2,1)}) fusion(f32[2,32,32,2048]{3,2,1,0:T(8,128)} %copy.247, f32[2,1024]{1,0:T(2,128)S(1)} %mul.567, f32[2,1024,2048,1]{2,1,3,0:T(8,128)} %get-tuple-element.136), kind=kLoop, calls=%fused_computation.7 | loop fusion | flops 16777216 | bytes 50339840 | tf_op jit(solution)/shard_map/convert_element_type | solution.py:166
  562.6 18.9 %fusion.16 = (bf16[2,2,1024,512]{3,2,1,0:T(8,128)(2,1)}, bf16[2,2,1024,512]{3,2,1,0:T(8,128)(2,1)S(1)}) fusion(f32[2,1024,2,512]{3,1,2,0:T(8,128)} %fusion.98, f32[2,1024,2,512]{3,1,2,0:T(8,128)} %get-tuple-element.134, bf16[2,2,512,2048]{3,2,1,0:T(8,128)(2,1)} %bitcast.296, bf16[2,1024,2048]{2,1,0:T(8,128)(2,1)} %get-tuple-element.122), kind=kOutput, calls=%fused_computation.29 | convolution fusion | flops 8617197568 | bytes 41943040 | tf_op jit(solution)/shard_map/erd,epfd->eprf/dot_general | solution.py:62
  581.5 16.2 %fusion.99 = f32[2,1024,2048,1]{2,1,3,0:T(8,128)} fusion(bf16[2,2,1024,512]{3,2,1,0:T(8,128)(2,1)S(1)} %get-tuple-element.98, bf16[2,2,2048,512]{3,2,1,0:T(8,128)(2,1)} %bitcast.298), kind=kOutput, calls=%fused_computation.182 | convolution fusion | flops 8589934592 | bytes 29360128 | tf_op jit(solution)/shard_map/eprf,epdf->erd/dot_general | solution.py:62
  597.6 16.9 %fusion.1 = bf16[2,1024,2048]{2,1,0:T(8,128)(2,1)} fusion(f32[2,1024,2048,1]{2,1,3,0:T(8,128)} %fusion.99, bf16[2,2,1024,512]{3,2,1,0:T(8,128)(2,1)} %get-tuple-element.97, bf16[2,2,2048,512]{3,2,1,0:T(8,128)(2,1)} %bitcast.300), kind=kOutput, calls=%fused_computation.4 | convolution fusion | flops 8598323200 | bytes 37748736 | tf_op jit(solution)/shard_map/eprf,epdf->erd/dot_general | solution.py:62
  614.6 10.7 bitcast_convert_fusion
  627.8 2.8 all-to-all-start.2
  630.7 11.0 all-to-all-done.2
  641.9 167.0 %reduce-scatter.8.cloned.1.call-done = bf16[128,2048]{1,0:T(8,128)(2,1)} async-done(((bf16[4096,2048]{1,0:T(8,128)(2,1)}), bf16[128,2048]{1,0:T(8,128)(2,1)}) %reduce-scatter.8.cloned.1.call-update) | async-done | bytes 524304 | tf_op jit(solution)/shard_map/reduce_scatter | solution.py:186
  808.9 1.8 multiply_reduce_fusion
  812.1 74.1 %all-gather.15.cloned.1.call-done = bf16[1024,2048]{1,0:T(8,128)(2,1)} async-done(((bf16[128,2048]{1,0:T(8,128)(2,1)}), bf16[1024,2048]{1,0:T(8,128)(2,1)}) %all-gather.15.cloned.1.call-update) | async-done | bytes 4194320 | tf_op jit(solution)/shard_map/all_gather | solution.py:211
  886.2 4.1 multiply_reduce_fusion.1
  890.3 5.9 fusion.39
  897.6 2.0 fusion.43
  903.2 2.0 copy.260
  906.2 6.8 fusion.47
  913.0 3.4 copy.262
  916.4 8.0 convolution_convert_fusion
  924.5 11.1 bitcast_convert_fusion.1
  937.0 16.9 %fusion.101 = f32[2,2,512,2048]{3,2,1,0:T(8,128)} fusion(bf16[2,2,1024,512]{3,2,1,0:T(8,128)(2,1)} %copy-done.34, bf16[2,1024,2048,1]{2,1,3,0:T(8,128)(2,1)} %bitcast.249), kind=kOutput, calls=%fused_computation.184 | convolution fusion | flops 8589934592 | bytes 29360128 | tf_op jit(solution)/shard_map/erd,eprf->epdf/dot_general | solution.py:62
  953.9 2.6 fusion.100
  956.6 16.5 %fusion.102 = f32[2,2,512,2048]{3,2,1,0:T(8,128)} fusion(bf16[2,2,1024,512]{3,2,1,0:T(8,128)(2,1)} %get-tuple-element.97, bf16[2,1024,2048,1]{2,1,3,0:T(8,128)(2,1)} %bitcast.250), kind=kOutput, calls=%fused_computation.185 | convolution fusion | flops 8589934592 | bytes 29360128 | tf_op jit(solution)/shard_map/erd,eprf->epdf/dot_general | solution.py:62
  973.9 5.7 all-to-all-start.3
  979.7 16.6 %fusion.9 = f32[2,2,512,2048]{3,2,1,0:T(8,128)} fusion(bf16[2,2,1024,512]{3,2,1,0:T(8,128)(2,1)} %copy-done.33, bf16[2,1024,2048]{2,1,0:T(8,128)(2,1)} %get-tuple-element.122), kind=kOutput, calls=%fused_computation.20 | convolution fusion | flops 8589934592 | bytes 29360128 | tf_op jit(solution)/shard_map/eprf,erd->epfd/dot_general | solution.py:62
  996.3 16.4 %copy.269 = f32[4,2048,512]{2,1,0:T(8,128)} copy(f32[4,2048,512]{1,2,0:T(8,128)} %bitcast.240) | data formatting | bytes 33554432
  1012.6 16.5 %copy.270 = f32[4,2048,512]{2,1,0:T(8,128)} copy(f32[4,2048,512]{1,2,0:T(8,128)} %bitcast.241) | data formatting | bytes 33554432
  1029.1 42.9 %all_gather.35 = bf16[4096,64]{0,1:T(8,128)(2,1)S(1)} all-gather(bf16[128,64]{0,1:T(8,128)(2,1)S(1)} %multiply_convert_fusion.2), channel_id=1, replica_groups=mesh['seq'=8,'fsdp'=4] {'seq','fsdp'}, dimensions={0}, use_global_device_ids=true | all-gather | bytes 540672 | tf_op jit(solution)/shard_map/all_gather | solution.py:204
  1072.0 2.6 fusion.57
  1074.6 21.2 %reduce-scatter.10.cloned.1.call-done = bf16[128,2048]{1,0:T(8,128)(2,1)} async-done(((bf16[1024,2048]{1,0:T(8,128)(2,1)}), bf16[128,2048]{1,0:T(8,128)(2,1)}) %reduce-scatter.10.cloned.1.call-update) | async-done | bytes 524304 | tf_op jit(solution)/shard_map/reduce_scatter | solution.py:225
  1095.9 1.6 fusion.51
  1097.6 45.8 %all-reduce = f32[2,32,64]{2,0,1:T(2,128)S(1)} all-reduce(f32[2,32,64]{2,0,1:T(2,128)S(1)} %pad_maximum_fusion.7), channel_id=9, replica_groups=mesh['seq'=8,'fsdp'=4] {'seq','fsdp'}, use_global_device_ids=true, to_apply=%region_27.28.clone | all-reduce | flops 4096 | bytes 32768
  1144.0 138.5 %reduce-scatter.6.cloned.1.call-done = bf16[128,2048]{1,0:T(8,128)(2,1)} async-done(((bf16[4096,2048]{1,0:T(8,128)(2,1)}), bf16[128,2048]{1,0:T(8,128)(2,1)}) %reduce-scatter.6.cloned.1.call-update) | async-done | bytes 524304 | tf_op jit(solution)/shard_map/reduce_scatter | solution.py:195
  1282.5 2.8 fusion.54
  1285.3 2.6 reshape.357
  1288.0 1.5 fusion.93
  1293.2 25.0 %reduce-scatter.14.cloned.1.call-done = f32[64,2048]{1,0:T(8,128)} async-done(((f32[256,2048]{1,0:T(8,128)}), f32[64,2048]{1,0:T(8,128)}) %reduce-scatter.14.cloned.1.call-update) | async-done | bytes 524304 | tf_op jit(solution)/shard_map/reduce_scatter | solution.py:213
  (168 shorter events, 36.0 us)
Async XLA Ops:
  7.2 67.9 %all-gather.19.cloned.1.call-start = ((), (), s32[]{:S(2)}) async-start(), calls=%async_computation.18 | async-start | bytes 4587520 | tf_op jit(solution)/shard_map/all_gather | solution.py:121
  44.7 105.3 %all-gather.17.cloned.1.call-start = ((), (), s32[]{:S(2)}) async-start(), calls=%async_computation.17 | async-start | bytes 4718592 | tf_op jit(solution)/shard_map/all_gather | solution.py:101
  45.5 185.9 %all-gather.11.cloned.1.call-start = ((), (), s32[]{:S(2)}) async-start(), calls=%async_computation.9 | async-start | bytes 8650752 | tf_op jit(solution)/shard_map/all_gather | solution.py:126
  46.2 301.5 %all-gather.21.cloned.1.call-start = ((), (), s32[]{:S(2)}) async-start(), calls=%async_computation.19 | async-start | bytes 17301504 | tf_op jit(solution)/shard_map/all_gather | solution.py:128
  46.8 416.2 %all-gather.13.cloned.1.call-start = ((), (), s32[]{:S(2)}) async-start(), calls=%async_computation.10 | async-start | bytes 17301504 | tf_op jit(solution)/shard_map/all_gather | solution.py:147
  49.9 121.3 %copy-start.6 = (f32[1024,64]{1,0:T(8,128)}, f32[1024,64]{1,0:T(8,128)S(1)}, u32[]{:S(2)}) copy-start(f32[1024,64]{1,0:T(8,128)S(1)} %get-tuple-element.126) | copy-start | bytes 786436
  77.7 1.8 copy-start.4
  80.2 72.9 %copy-start.22 = (f32[2048]{0:T(1024)}, f32[2048]{0:T(1024)S(1)}, u32[]{:S(2)}) copy-start(f32[2048]{0:T(1024)S(1)} %get-tuple-element.85) | copy-start | bytes 24580
  80.2 156.0 %copy-start.20 = (f32[2048]{0:T(1024)}, f32[2048]{0:T(1024)S(1)}, u32[]{:S(2)}) copy-start(f32[2048]{0:T(1024)S(1)} %get-tuple-element.84) | copy-start | bytes 24580
  153.1 0.6 copy-start.28
  160.4 23.6 %copy-start.10 = (bf16[1024,256]{0,1:T(8,128)(2,1)}, bf16[1024,256]{0,1:T(8,128)(2,1)S(1)}, u32[]{:S(2)}) copy-start(bf16[1024,256]{0,1:T(8,128)(2,1)S(1)} %slice.127) | copy-start | bytes 1572868
  184.0 47.4 %copy-start.2 = (bf16[1,128,2048]{2,1,0:T(8,128)(2,1)S(1)}, bf16[1,128,2048]{2,1,0:T(8,128)(2,1)}, u32[]{:S(2)}) copy-start(bf16[1,128,2048]{2,1,0:T(8,128)(2,1)} %param.13) | copy-start | bytes 1572868
  188.2 0.8 copy-start.17
  231.4 6.8 copy-start.24
  236.2 1.0 copy-start
  236.2 42.8 %copy-start.30 = (f32[128]{0:T(128)}, f32[128]{0:T(128)S(1)}, u32[]{:S(2)}) copy-start(f32[128]{0:T(128)S(1)} %get-tuple-element.129) | copy-start | bytes 1540
  236.2 42.8 %copy-start.26 = (f32[128]{0:T(128)}, f32[128]{0:T(128)S(1)}, u32[]{:S(2)}) copy-start(f32[128]{0:T(128)S(1)} %fusion.86) | copy-start | bytes 1540
  238.1 570.7 %reduce-scatter.8.cloned.1.call-start = ((), (), s32[]{:S(2)}) async-start(), calls=%async_computation.12 | async-start | bytes 17301504 | tf_op jit(solution)/shard_map/reduce_scatter | solution.py:186
  480.7 15.8 %copy-start.5 = (bf16[2,32,32,2048]{3,2,1,0:T(8,128)(2,1)S(1)}, bf16[2,32,32,2048]{3,2,1,0:T(8,128)(2,1)}, u32[]{:S(2)}) copy-start(bf16[2,32,32,2048]{3,2,1,0:T(8,128)(2,1)} %copy.245) | copy-start | bytes 25165828
  511.4 19.9 %copy-start.33 = (bf16[2,2,1024,512]{3,2,1,0:T(8,128)(2,1)}, bf16[2,2,1024,512]{3,2,1,0:T(8,128)(2,1)S(1)}, u32[]{:S(2)}) copy-start(bf16[2,2,1024,512]{3,2,1,0:T(8,128)(2,1)S(1)} %get-tuple-element.133) | copy-start | bytes 12582916
  581.5 16.2 %copy-start.34 = (bf16[2,2,1024,512]{3,2,1,0:T(8,128)(2,1)}, bf16[2,2,1024,512]{3,2,1,0:T(8,128)(2,1)S(1)}, u32[]{:S(2)}) copy-start(bf16[2,2,1024,512]{3,2,1,0:T(8,128)(2,1)S(1)} %get-tuple-element.98) | copy-start | bytes 12582916
  625.3 1.0 copy-start.8
  625.3 16.3 %copy-start.25 = (s32[1,128,8]{1,2,0:T(8,128)S(1)}, s32[1,128,8]{1,2,0:T(8,128)}, u32[]{:S(2)}) copy-start(s32[1,128,8]{1,2,0:T(8,128)} %param.15) | copy-start | bytes 12292
  625.3 183.5 %copy-start.1 = (f32[128,2048]{1,0:T(8,128)S(1)}, f32[128,2048]{1,0:T(8,128)}, u32[]{:S(2)}) copy-start(f32[128,2048]{1,0:T(8,128)} %copy-done) | copy-start | bytes 3145732
  625.3 183.5 %copy-start.21 = (f32[2048]{0:T(1024)S(1)}, f32[2048]{0:T(1024)}, u32[]{:S(2)}) copy-start(f32[2048]{0:T(1024)} %copy-done.20) | copy-start | bytes 24580
  625.3 183.5 %copy-start.27 = (f32[128]{0:T(128)S(1)}, f32[128]{0:T(128)}, u32[]{:S(2)}) copy-start(f32[128]{0:T(128)} %copy-done.26) | copy-start | bytes 1540
  625.3 185.3 %copy-start.31 = (f32[128]{0:T(128)S(1)}, f32[128]{0:T(128)}, u32[]{:S(2)}) copy-start(f32[128]{0:T(128)} %copy-done.30) | copy-start | bytes 1540
  625.4 185.3 %copy-start.9 = (bf16[1,128,2048]{2,1,0:T(8,128)(2,1)S(1)}, bf16[1,128,2048]{2,1,0:T(8,128)(2,1)}, u32[]{:S(2)}) copy-start(bf16[1,128,2048]{2,1,0:T(8,128)(2,1)} %param.14) | copy-start | bytes 1572868
  627.8 13.9 %all-to-all-start.2 = ((f32[32,2,128]{2,1,0:T(2,128)}), f32[32,2,128]{2,1,0:T(2,128)S(1)}, u32[]{:S(2)}, u32[]{:S(2)}) async-start(f32[32,2,128]{2,1,0:T(2,128)} %get-tuple-element.92), calls=%async_computation.4 | async-start | bytes 65536 | tf_op jit(solution)/shard_map/all_to_all | solution.py:191
  630.6 255.6 %all-gather.15.cloned.1.call-start = ((), (), s32[]{:S(2)}) async-start(), calls=%async_computation.13 | async-start | bytes 4718592 | tf_op jit(solution)/shard_map/all_gather | solution.py:211
  811.9 162.1 %reduce-scatter.12.cloned.1.call-start = ((), (), s32[]{:S(2)}) async-start(), calls=%async_computation.15 | async-start | bytes 7864320 | tf_op jit(solution)/shard_map/reduce_scatter | solution.py:230
  812.1 84.1 %copy-start.11 = (bf16[1024,256]{0,1:T(8,128)(2,1)S(1)}, bf16[1024,256]{0,1:T(8,128)(2,1)}, u32[]{:S(2)}) copy-start(bf16[1024,256]{0,1:T(8,128)(2,1)} %copy-done.10) | copy-start | bytes 1572868
  886.2 9.9 slice-start
  890.3 5.9 slice-start.1
  896.2 1.4 copy-start.14
  896.2 1.4 copy-start.15
  896.2 3.4 copy-start.12
  896.2 3.4 copy-start.13
  897.6 3.4 copy-start.7
  897.6 3.4 copy-start.16
  899.7 6.6 copy-start.23
  899.7 6.5 copy-start.29
  913.0 3.5 copy-start.19
  916.4 179.5 %reduce-scatter.10.cloned.1.call-start = ((), (), s32[]{:S(2)}) async-start(), calls=%async_computation.14 | async-start | bytes 4718592 | tf_op jit(solution)/shard_map/reduce_scatter | solution.py:225
  924.5 358.0 %reduce-scatter.6.cloned.1.call-start = ((), (), s32[]{:S(2)}) async-start(), calls=%async_computation.11 | async-start | bytes 17301504 | tf_op jit(solution)/shard_map/reduce_scatter | solution.py:195
  935.6 1.2 copy-start.3
  935.6 382.6 %reduce-scatter.14.cloned.1.call-start = ((), (), s32[]{:S(2)}) async-start(), calls=%async_computation.16 | async-start | bytes 2621440 | tf_op jit(solution)/shard_map/reduce_scatter | solution.py:213
  937.0 17.0 %copy-start.18 = (bf16[2,128,1024]{2,1,0:T(8,128)(2,1)S(1)}, bf16[2,128,1024]{2,1,0:T(8,128)(2,1)}, u32[]{:S(2)}) copy-start(bf16[2,128,1024]{2,1,0:T(8,128)(2,1)} %copy-done.17) | copy-start | bytes 1572868
  937.0 17.0 %copy-start.32 = (bf16[1024,2048]{1,0:T(8,128)(2,1)S(1)}, bf16[1024,2048]{1,0:T(8,128)(2,1)}, u32[]{:S(2)}) copy-start(bf16[1024,2048]{1,0:T(8,128)(2,1)} %all-gather.15.cloned.1.call-done) | copy-start | bytes 12582916
  973.9 311.4 %all-to-all-start.3 = ((f32[8,64,768]{2,1,0:T(8,128)}), f32[8,64,768]{2,1,0:T(8,128)}, u32[]{:S(2)}, u32[]{:S(2)}) async-start(f32[8,64,768]{2,1,0:T(8,128)} %bitcast.270), calls=%async_computation.7 | async-start | bytes 3145728 | tf_op jit(solution)/shard_map/all_to_all | solution.py:231
Sparse Core Ops, SparseCore 0:
  44.9 30.1 all-gather.18
  77.2 72.7 all-gather.16
  152.9 78.4 all-gather.10
  234.1 113.5 all-gather.20
  350.5 112.5 all-gather.12
  625.5 183.2 reduce-scatter.7
  812.0 74.2 all-gather.14
  916.5 57.3 reduce-scatter.11
  977.6 118.2 reduce-scatter.9
  1098.0 184.4 reduce-scatter.5
  1285.6 32.5 reduce-scatter.13
where the time goes:
time: 1340 us; the launch traced here: 1320 us
  waiting for transfers between devices  719 us (54%)
  matrix products  265 us (20%)
  blocking collectives  188 us (14%)
  local copies, waits for them, and re-layouts  88.1 us (7%)
  other arithmetic  40.5 us (3%)
  between operations  14.8 us (1%)
    dot_general x19, matrix products, ein(): return jnp.einsum(spec, *args, preferred_element_type=f32)  206 us
    reduce_scatter x1, waiting for transfers between devices, body(): lax.psum_scatter(spread(back), AXES, scatter_dimension=0, tiled=True)  167 us
    reduce_scatter x1, waiting for transfers between devices, body(): lax.psum_scatter(spread(w_rows * out), AXES, scatter_dimension=0, tiled=T...  139 us
    all_gather x1, waiting for transfers between devices, body(): x_all = lax.all_gather(normed_mid, AXES, axis=0, tiled=True)  102 us
    all_gather x1, waiting for transfers between devices, body(): lax.all_gather(resid_grad.astype(bf16), 'seq', axis=0, tiled=True)  74.1 us
    all_gather x1, waiting for transfers between devices, body(): x_seq = lax.all_gather(x_own, 'seq', axis=0, tiled=True)  69.8 us
    all_gather x1, waiting for transfers between devices, body(): cot_all = lax.all_gather(cot_own, AXES, axis=0, tiled=True)  68.4 us
    unnamed x88, local copies, waits for them, and re-layouts  51 us
  transfers between devices with their start and end apart: 13, of which 12 were waited for; matrix products, arithmetic and copies ran while one was open for 14% of the time, Pallas kernels for 0%

commit v1 on v0

--- a/solution.py
+++ b/solution.py
@@ -98,7 +98,23 @@
     cot_own = cotangent[0]
     chosen = routes[0]
     routes_all = lax.all_gather(chosen, AXES, axis=0, tiled=True)
-    x_seq = lax.all_gather(x_own, "seq", axis=0, tiled=True)
+    count, mine, rows = (lax.axis_size("seq"), lax.axis_index("seq"), x_own.shape[0])
+    forward = [(i, (i + 1) % count) for i in range(count)]
+    behind = [(i, (i - 1) % count) for i in range(count)]
+    x_seq = jnp.zeros((*x_own.shape[:0], count * rows, *x_own.shape[0 + 1 :]), x_own.dtype)
+    x_seq = lax.dynamic_update_slice_in_dim(x_seq, x_own, mine * rows, axis=0)
+    from_left = from_right = x_own
+    middle = count // 2
+    for step in range(1, middle + 1):
+        from_left = lax.ppermute(from_left, "seq", forward)
+        x_seq = lax.dynamic_update_slice_in_dim(
+            x_seq, from_left, (mine - step) % count * rows, axis=0
+        )
+        if step < count - middle:
+            from_right = lax.ppermute(from_right, "seq", behind)
+            x_seq = lax.dynamic_update_slice_in_dim(
+                x_seq, from_right, (mine + step) % count * rows, axis=0
+            )
     small = jnp.concatenate(
         [
             router_weight,

time: 1340 us -> 1280 us (0.955)
  waiting for transfers between devices: 719 us -> 650 us
  starting transfers between devices: 9.6 us -> 26.3 us
    all_gather x1 -> x0, waiting for transfers between devices: 69.8 us -> none  [body(): x_seq = lax.all_gather(x_own, 'seq', axis=0, tiled=True)]
    ppermute x0 -> x7, waiting for transfers between devices: none -> 67.9 us  [the longest x4 61.1 us: body(): from_left = lax.ppermute(from_left, 'seq', forward)]
    all_gather x1, waiting for transfers between devices: 68.4 us -> 42.4 us  [body(): cot_all = lax.all_gather(cot_own, AXES, axis=0, tiled=True)]
    all_gather x1, waiting for transfers between devices: 25.2 us -> 0.02 us  [body(): lax.all_gather(moved, 'fsdp', axis=1).reshape(width, 3 * cols + 128)]
    ppermute x0 -> x7, starting transfers between devices: none -> 16.9 us  [the longest x4 8.74 us: body(): from_left = lax.ppermute(from_left, 'seq', forward)]
    all_gather x1, waiting for transfers between devices: 14.1 us -> 0.01 us  [body(): out_full = lax.all_gather(output_weight, AXES, axis=0, tiled=True)]
    unnamed x88 -> x90, local copies, waits for them, and re-layouts: 51 us -> 49.9 us
  transfers between devices with their start and end apart: 13 -> 19, of which waited for: 12 -> 14; matrix products, arithmetic and copies ran while one was open for 14% -> 15% of each run, Pallas kernels for 0% -> 0%
where the time goes in v1:
time: 1280 us
  waiting for transfers between devices  650 us (51%)
  matrix products  264 us (21%)
  blocking collectives  183 us (14%)
  local copies, waits for them, and re-layouts  96.1 us (8%)
  other arithmetic  40.6 us (3%)
  starting transfers between devices  26.3 us (2%)
  between operations  15.1 us (1%)
    dot_general x19, matrix products, ein(): return jnp.einsum(spec, *args, preferred_element_type=f32)  205 us
    reduce_scatter x1, waiting for transfers between devices, body(): lax.psum_scatter(spread(back), AXES, scatter_dimension=0, tiled=True)  166 us
    reduce_scatter x1, waiting for transfers between devices, body(): lax.psum_scatter(spread(w_rows * out), AXES, scatter_dimension=0, tiled=T...  139 us
    all_gather x1, waiting for transfers between devices, body(): x_all = lax.all_gather(normed_mid, AXES, axis=0, tiled=True)  102 us
    all_gather x1, waiting for transfers between devices, body(): lax.all_gather(resid_grad.astype(bf16), 'seq', axis=0, tiled=True)  74.1 us
    ppermute x4, waiting for transfers between devices, body(): from_left = lax.ppermute(from_left, 'seq', forward)  61.1 us
    unnamed x90, local copies, waits for them, and re-layouts  49.9 us
    unnamed x1, blocking collectives  45.3 us
  transfers between devices with their start and end apart: 19, of which 14 were waited for; matrix products, arithmetic and copies ran while one was open for 15% of the time, Pallas kernels for 0%

profile of v1, /device:TPU:0, one launch (start us, length us, event | category | flops | bytes accessed | tf_op | source)
XLA Modules:
  0.0 1275.6 jit_solution(10258727008049498208)
XLA Ops:
  13.0 30.4 %all_to_all.34 = bf16[8,64,896]{2,1,0:T(8,128)(2,1)S(1)} all-to-all(bf16[8,64,896]{2,1,0:T(8,128)(2,1)S(1)} %copy.233), channel_id=1, replica_groups=mesh['seq'=8,'fsdp'=4] {'seq'}, dimensions={0} | all-to-all | bytes 1835008 | tf_op jit(solution)/shard_map/all_to_all | solution.py:136
  47.5 3.6 collective-permute-start.1
  51.1 18.0 %collective-permute-done = bf16[128,2048]{1,0:T(8,128)(2,1)S(1)} collective-permute-done((bf16[128,2048]{1,0:T(8,128)(2,1)S(1)}, bf16[128,2048]{1,0:T(8,128)(2,1)S(1)}, u32[]{:S(2)}, u32[]{:S(2)}) %collective-permute-start) | collective-permute-done | bytes 524320 | tf_op jit(solution)/shard_map/ppermute | solution.py:109
  69.1 2.5 collective-permute-start.2
  71.6 2.5 broadcast_in_dim.58
  75.0 2.3 collective-permute-start.3
  77.3 3.0 fusion.80
  80.3 14.1 %collective-permute-done.2 = bf16[128,2048]{1,0:T(8,128)(2,1)S(1)} collective-permute-done((bf16[128,2048]{1,0:T(8,128)(2,1)S(1)}, bf16[128,2048]{1,0:T(8,128)(2,1)S(1)}, u32[]{:S(2)}, u32[]{:S(2)}) %collective-permute-start.2) | collective-permute-done | bytes 524320 | tf_op jit(solution)/shard_map/ppermute | solution.py:109
  94.5 2.5 collective-permute-start.4
  98.7 2.2 collective-permute-start.5
  101.7 16.4 %collective-permute-done.4 = bf16[128,2048]{1,0:T(8,128)(2,1)S(1)} collective-permute-done((bf16[128,2048]{1,0:T(8,128)(2,1)S(1)}, bf16[128,2048]{1,0:T(8,128)(2,1)S(1)}, u32[]{:S(2)}, u32[]{:S(2)}) %collective-permute-start.4) | collective-permute-done | bytes 524320 | tf_op jit(solution)/shard_map/ppermute | solution.py:109
  118.1 2.6 collective-permute-start.6
  122.4 6.7 collective-permute-done.5
  130.0 12.6 collective-permute-done.6
  143.4 3.1 fusion.5
  146.5 2.6 copy.235
  151.0 5.8 fusion.30
  163.7 2.4 copy.296
  167.4 3.6 subtract_convert_fusion.3
  171.0 9.3 fusion.8
  180.3 4.1 fusion.36
  185.2 24.9 %all_to_all.35 = bf16[8,128,256]{1,2,0:T(8,128)(2,1)S(1)} all-to-all(bf16[8,128,256]{1,2,0:T(8,128)(2,1)S(1)} %copy.241), channel_id=1, replica_groups=mesh['seq'=8,'fsdp'=4] {'seq'}, dimensions={0} | all-to-all | bytes 1048576 | tf_op jit(solution)/shard_map/all_to_all | solution.py:159
  210.1 4.8 multiply_reduce_fusion.3
  216.9 40.1 %all-gather.1 = s32[1,4096,8]{1,2,0:T(8,128)S(1)} all-gather(s32[1,128,8]{1,2,0:T(8,128)S(1)} %copy-done.25), channel_id=3, replica_groups=mesh['seq'=8,'fsdp'=4] {'seq','fsdp'}, dimensions={1}, use_global_device_ids=true | all-gather | bytes 135168 | tf_op jit(solution)/shard_map/all_gather | solution.py:100
  257.4 42.4 %all-gather.17.cloned.1.call-done = bf16[1,4096,2048]{2,1,0:T(8,128)(2,1)} async-done(((bf16[1,128,2048]{2,1,0:T(8,128)(2,1)}), bf16[1,4096,2048]{2,1,0:T(8,128)(2,1)}) %all-gather.17.cloned.1.call-update) | async-done | bytes 16777232 | tf_op jit(solution)/shard_map/all_gather | solution.py:144
  299.8 7.0 convolution_bitcast_fusion
  306.8 6.2 copy.247
  313.1 102.0 %all-gather.11.cloned.1.call-done = bf16[4096,2048]{1,0:T(8,128)(2,1)} async-done(((bf16[128,2048]{1,0:T(8,128)(2,1)}), bf16[4096,2048]{1,0:T(8,128)(2,1)}) %all-gather.11.cloned.1.call-update) | async-done | bytes 16777232 | tf_op jit(solution)/shard_map/all_gather | solution.py:163
  415.1 9.4 convert_bitcast_fusion
  424.5 8.3 copy.245
  432.7 15.8 %fusion.98 = f32[2,1024,2,512]{3,1,2,0:T(8,128)} fusion(bf16[2,1024,2048,1]{2,1,3,0:T(8,128)(2,1)} %bitcast.244, bf16[2,2,2048,512]{3,2,1,0:T(8,128)(2,1)} %bitcast.293), kind=kOutput, calls=%fused_computation.189 | convolution fusion | flops 8589934592 | bytes 25165824 | tf_op jit(solution)/shard_map/erd,epdf->eprf/dot_general | solution.py:62
  448.5 15.0 %fusion.17 = (bf16[2,2,1024,512]{3,2,1,0:T(8,128)(2,1)S(1)}, f32[2,1024,2,512]{3,1,2,0:T(8,128)}) fusion(f32[2,1024,2,512]{3,1,2,0:T(8,128)} %fusion.98, bf16[2,1024,2048,1]{2,1,3,0:T(8,128)(2,1)S(1)} %bitcast.247, bf16[2,2,2048,512]{3,2,1,0:T(8,128)(2,1)} %bitcast.295), kind=kOutput, calls=%fused_computation.31 | convolution fusion | flops 8602517504 | bytes 37748736 | tf_op jit(solution)/shard_map/erd,epdf->eprf/dot_general | solution.py:62
  463.5 19.9 %fusion.3 = (f32[2,1024]{1,0:T(2,128)S(1)}, f32[2,1024,2048,1]{2,1,3,0:T(8,128)}) fusion(f32[2,32,32,2048]{3,2,1,0:T(8,128)} %copy.247, bf16[2,2,1024,512]{3,2,1,0:T(8,128)(2,1)S(1)} %get-tuple-element.133, bf16[2,2,512,2048]{3,2,1,0:T(8,128)(2,1)} %bitcast.291), kind=kOutput, calls=%fused_computation.8 | convolution fusion | flops 8598321152 | bytes 46145536 | tf_op jit(solution)/shard_map/eprf,epfd->erd/dot_general | solution.py:62
  483.5 11.0 fusion.97
  497.7 17.0 %fusion.2 = (bf16[2,1024,2048]{2,1,0:T(8,128)(2,1)}, bf16[2,1024,2048]{2,1,0:T(8,128)(2,1)}) fusion(f32[2,32,32,2048]{3,2,1,0:T(8,128)} %copy.247, f32[2,1024]{1,0:T(2,128)S(1)} %mul.599, f32[2,1024,2048,1]{2,1,3,0:T(8,128)} %get-tuple-element.136), kind=kLoop, calls=%fused_computation.7 | loop fusion | flops 16777216 | bytes 50339840 | tf_op jit(solution)/shard_map/convert_element_type | solution.py:182
  514.6 18.7 %fusion.16 = (bf16[2,2,1024,512]{3,2,1,0:T(8,128)(2,1)}, bf16[2,2,1024,512]{3,2,1,0:T(8,128)(2,1)S(1)}) fusion(f32[2,1024,2,512]{3,1,2,0:T(8,128)} %fusion.98, f32[2,1024,2,512]{3,1,2,0:T(8,128)} %get-tuple-element.134, bf16[2,2,512,2048]{3,2,1,0:T(8,128)(2,1)} %bitcast.292, bf16[2,1024,2048]{2,1,0:T(8,128)(2,1)} %get-tuple-element.122), kind=kOutput, calls=%fused_computation.29 | convolution fusion | flops 8617197568 | bytes 41943040 | tf_op jit(solution)/shard_map/erd,epfd->eprf/dot_general | solution.py:62
  533.3 16.2 %fusion.99 = f32[2,1024,2048,1]{2,1,3,0:T(8,128)} fusion(bf16[2,2,1024,512]{3,2,1,0:T(8,128)(2,1)S(1)} %get-tuple-element.98, bf16[2,2,2048,512]{3,2,1,0:T(8,128)(2,1)} %bitcast.294), kind=kOutput, calls=%fused_computation.190 | convolution fusion | flops 8589934592 | bytes 29360128 | tf_op jit(solution)/shard_map/eprf,epdf->erd/dot_general | solution.py:62
  549.5 16.9 %fusion.1 = bf16[2,1024,2048]{2,1,0:T(8,128)(2,1)} fusion(f32[2,1024,2048,1]{2,1,3,0:T(8,128)} %fusion.99, bf16[2,2,1024,512]{3,2,1,0:T(8,128)(2,1)} %get-tuple-element.97, bf16[2,2,2048,512]{3,2,1,0:T(8,128)(2,1)} %bitcast.296), kind=kOutput, calls=%fused_computation.4 | convolution fusion | flops 8598323200 | bytes 37748736 | tf_op jit(solution)/shard_map/eprf,epdf->erd/dot_general | solution.py:62
  566.5 10.7 bitcast_convert_fusion
  579.6 2.8 all-to-all-start.2
  582.5 11.0 all-to-all-done.2
  593.7 165.6 %reduce-scatter.8.cloned.1.call-done = bf16[128,2048]{1,0:T(8,128)(2,1)} async-done(((bf16[4096,2048]{1,0:T(8,128)(2,1)}), bf16[128,2048]{1,0:T(8,128)(2,1)}) %reduce-scatter.8.cloned.1.call-update) | async-done | bytes 524304 | tf_op jit(solution)/shard_map/reduce_scatter | solution.py:202
  762.7 74.1 %all-gather.13.cloned.1.call-done = bf16[1024,2048]{1,0:T(8,128)(2,1)} async-done(((bf16[128,2048]{1,0:T(8,128)(2,1)}), bf16[1024,2048]{1,0:T(8,128)(2,1)}) %all-gather.13.cloned.1.call-update) | async-done | bytes 4194320 | tf_op jit(solution)/shard_map/all_gather | solution.py:227
  836.7 4.1 multiply_reduce_fusion.1
  840.8 5.9 fusion.39
  856.7 6.9 fusion.47
  863.7 3.4 copy.262
  867.1 8.0 convolution_convert_fusion
  875.2 11.1 bitcast_convert_fusion.1
  887.7 16.9 %fusion.101 = f32[2,2,512,2048]{3,2,1,0:T(8,128)} fusion(bf16[2,2,1024,512]{3,2,1,0:T(8,128)(2,1)} %copy-done.35, bf16[2,1024,2048,1]{2,1,3,0:T(8,128)(2,1)} %bitcast.245), kind=kOutput, calls=%fused_computation.192 | convolution fusion | flops 8589934592 | bytes 29360128 | tf_op jit(solution)/shard_map/erd,eprf->epdf/dot_general | solution.py:62
  904.6 2.6 fusion.100
  907.3 16.5 %fusion.102 = f32[2,2,512,2048]{3,2,1,0:T(8,128)} fusion(bf16[2,2,1024,512]{3,2,1,0:T(8,128)(2,1)} %get-tuple-element.97, bf16[2,1024,2048,1]{2,1,3,0:T(8,128)(2,1)} %bitcast.246), kind=kOutput, calls=%fused_computation.193 | convolution fusion | flops 8589934592 | bytes 29360128 | tf_op jit(solution)/shard_map/erd,eprf->epdf/dot_general | solution.py:62
  924.6 5.8 all-to-all-start.3
  930.4 16.6 %fusion.9 = f32[2,2,512,2048]{3,2,1,0:T(8,128)} fusion(bf16[2,2,1024,512]{3,2,1,0:T(8,128)(2,1)} %copy-done.34, bf16[2,1024,2048]{2,1,0:T(8,128)(2,1)} %get-tuple-element.122), kind=kOutput, calls=%fused_computation.20 | convolution fusion | flops 8589934592 | bytes 29360128 | tf_op jit(solution)/shard_map/eprf,erd->epfd/dot_general | solution.py:62
  947.0 16.4 %copy.269 = f32[4,2048,512]{2,1,0:T(8,128)} copy(f32[4,2048,512]{1,2,0:T(8,128)} %bitcast.234) | data formatting | bytes 33554432
  963.3 16.4 %copy.270 = f32[4,2048,512]{2,1,0:T(8,128)} copy(f32[4,2048,512]{1,2,0:T(8,128)} %bitcast.235) | data formatting | bytes 33554432
  979.8 42.8 %all_gather.31 = bf16[4096,64]{0,1:T(8,128)(2,1)S(1)} all-gather(bf16[128,64]{0,1:T(8,128)(2,1)S(1)} %multiply_convert_fusion.2), channel_id=1, replica_groups=mesh['seq'=8,'fsdp'=4] {'seq','fsdp'}, dimensions={0}, use_global_device_ids=true | all-gather | bytes 540672 | tf_op jit(solution)/shard_map/all_gather | solution.py:220
  1022.6 2.6 fusion.57
  1025.2 21.3 %reduce-scatter.10.cloned.1.call-done = bf16[128,2048]{1,0:T(8,128)(2,1)} async-done(((bf16[1024,2048]{1,0:T(8,128)(2,1)}), bf16[128,2048]{1,0:T(8,128)(2,1)}) %reduce-scatter.10.cloned.1.call-update) | async-done | bytes 524304 | tf_op jit(solution)/shard_map/reduce_scatter | solution.py:241
  1048.3 45.3 %all-reduce = f32[2,32,64]{2,0,1:T(2,128)S(1)} all-reduce(f32[2,32,64]{2,0,1:T(2,128)S(1)} %pad_maximum_fusion.7), channel_id=8, replica_groups=mesh['seq'=8,'fsdp'=4] {'seq','fsdp'}, use_global_device_ids=true, to_apply=%region_27.28.clone | all-reduce | flops 4096 | bytes 32768
  1094.1 138.9 %reduce-scatter.6.cloned.1.call-done = bf16[128,2048]{1,0:T(8,128)(2,1)} async-done(((bf16[4096,2048]{1,0:T(8,128)(2,1)}), bf16[128,2048]{1,0:T(8,128)(2,1)}) %reduce-scatter.6.cloned.1.call-update) | async-done | bytes 524304 | tf_op jit(solution)/shard_map/reduce_scatter | solution.py:211
  1233.0 2.8 fusion.54
  1235.9 2.6 reshape.357
  1243.8 24.8 %reduce-scatter.14.cloned.1.call-done = f32[64,2048]{1,0:T(8,128)} async-done(((f32[256,2048]{1,0:T(8,128)}), f32[64,2048]{1,0:T(8,128)}) %reduce-scatter.14.cloned.1.call-update) | async-done | bytes 524304 | tf_op jit(solution)/shard_map/reduce_scatter | solution.py:229
  (190 shorter events, 58.8 us)
Async XLA Ops:
  7.2 39.2 %copy-start.2 = (bf16[1,128,2048]{2,1,0:T(8,128)(2,1)S(1)}, bf16[1,128,2048]{2,1,0:T(8,128)(2,1)}, u32[]{:S(2)}) copy-start(bf16[1,128,2048]{2,1,0:T(8,128)(2,1)} %param.13) | copy-start | bytes 1572868
  7.2 139.3 %all-gather.15.cloned.1.call-start = ((), (), s32[]{:S(2)}) async-start(), calls=%async_computation.17 | async-start | bytes 4587520 | tf_op jit(solution)/shard_map/all_gather | solution.py:137
  44.8 165.3 %all-gather.9.cloned.1.call-start = ((), (), s32[]{:S(2)}) async-start(), calls=%async_computation.9 | async-start | bytes 8650752 | tf_op jit(solution)/shard_map/all_gather | solution.py:142
  45.6 254.2 %all-gather.17.cloned.1.call-start = ((), (), s32[]{:S(2)}) async-start(), calls=%async_computation.18 | async-start | bytes 17301504 | tf_op jit(solution)/shard_map/all_gather | solution.py:144
  46.3 368.8 %all-gather.11.cloned.1.call-start = ((), (), s32[]{:S(2)}) async-start(), calls=%async_computation.10 | async-start | bytes 17301504 | tf_op jit(solution)/shard_map/all_gather | solution.py:163
  46.4 22.8 %collective-permute-start = (bf16[128,2048]{1,0:T(8,128)(2,1)S(1)}, bf16[128,2048]{1,0:T(8,128)(2,1)S(1)}, u32[]{:S(2)}, u32[]{:S(2)}) collective-permute-start(bf16[128,2048]{1,0:T(8,128)(2,1)S(1)} %bitcast.236), channel_id=1, source_target_pairs={{0,4},{4,8},{8,12},{12,16},{16,20},{20,24},{24,28},{28,0},{1,5},{5... | collective-permute-start | bytes 1572872 | tf_op jit(solution)/shard_map/ppermute | solution.py:109
  47.5 27.5 %collective-permute-start.1 = (bf16[128,2048]{1,0:T(8,128)(2,1)S(1)}, bf16[128,2048]{1,0:T(8,128)(2,1)S(1)}, u32[]{:S(2)}, u32[]{:S(2)}) collective-permute-start(bf16[128,2048]{1,0:T(8,128)(2,1)S(1)} %bitcast.237), channel_id=1, source_target_pairs={{0,28},{4,0},{8,4},{12,8},{16,12},{20,16},{24,20},{28,24},{1,29},{... | collective-permute-start | bytes 1572872 | tf_op jit(solution)/shard_map/ppermute | solution.py:114
  69.1 25.3 %collective-permute-start.2 = (bf16[128,2048]{1,0:T(8,128)(2,1)S(1)}, bf16[128,2048]{1,0:T(8,128)(2,1)S(1)}, u32[]{:S(2)}, u32[]{:S(2)}) collective-permute-start(bf16[128,2048]{1,0:T(8,128)(2,1)S(1)} %collective-permute-done), channel_id=1, source_target_pairs={{0,4},{4,8},{8,12},{12,16},{16,20},{20,24},{24,28},{28,0},{1,5},{5... | collective-permute-start | bytes 1572872 | tf_op jit(solution)/shard_map/ppermute | solution.py:109
  75.0 23.7 %collective-permute-start.3 = (bf16[128,2048]{1,0:T(8,128)(2,1)S(1)}, bf16[128,2048]{1,0:T(8,128)(2,1)S(1)}, u32[]{:S(2)}, u32[]{:S(2)}) collective-permute-start(bf16[128,2048]{1,0:T(8,128)(2,1)S(1)} %collective-permute-done.1), channel_id=1, source_target_pairs={{0,28},{4,0},{8,4},{12,8},{16,12},{20,16},{24,20},{28,24},{1,29},{... | collective-permute-start | bytes 1572872 | tf_op jit(solution)/shard_map/ppermute | solution.py:114
  80.3 87.0 %copy-start.6 = (f32[1024,64]{1,0:T(8,128)}, f32[1024,64]{1,0:T(8,128)S(1)}, u32[]{:S(2)}) copy-start(f32[1024,64]{1,0:T(8,128)S(1)} %get-tuple-element.126) | copy-start | bytes 786436
  94.5 23.7 %collective-permute-start.4 = (bf16[128,2048]{1,0:T(8,128)(2,1)S(1)}, bf16[128,2048]{1,0:T(8,128)(2,1)S(1)}, u32[]{:S(2)}, u32[]{:S(2)}) collective-permute-start(bf16[128,2048]{1,0:T(8,128)(2,1)S(1)} %collective-permute-done.2), channel_id=1, source_target_pairs={{0,4},{4,8},{8,12},{12,16},{16,20},{20,24},{24,28},{28,0},{1,5},{5... | collective-permute-start | bytes 1572872 | tf_op jit(solution)/shard_map/ppermute | solution.py:109
  98.7 30.5 %collective-permute-start.5 = (bf16[128,2048]{1,0:T(8,128)(2,1)S(1)}, bf16[128,2048]{1,0:T(8,128)(2,1)S(1)}, u32[]{:S(2)}, u32[]{:S(2)}) collective-permute-start(bf16[128,2048]{1,0:T(8,128)(2,1)S(1)} %collective-permute-done.3), channel_id=1, source_target_pairs={{0,28},{4,0},{8,4},{12,8},{16,12},{20,16},{24,20},{28,24},{1,29},{... | collective-permute-start | bytes 1572872 | tf_op jit(solution)/shard_map/ppermute | solution.py:114
  118.1 24.4 %collective-permute-start.6 = (bf16[128,2048]{1,0:T(8,128)(2,1)S(1)}, bf16[128,2048]{1,0:T(8,128)(2,1)S(1)}, u32[]{:S(2)}, u32[]{:S(2)}) collective-permute-start(bf16[128,2048]{1,0:T(8,128)(2,1)S(1)} %collective-permute-done.4), channel_id=1, source_target_pairs={{0,4},{4,8},{8,12},{12,16},{16,20},{20,24},{24,28},{28,0},{1,5},{5... | collective-permute-start | bytes 1572872 | tf_op jit(solution)/shard_map/ppermute | solution.py:109
  146.5 3.4 copy-start.29
  149.2 7.6 copy-start.4
  149.9 1.1 copy-start.23
  149.9 65.1 %copy-start.21 = (f32[2048]{0:T(1024)}, f32[2048]{0:T(1024)S(1)}, u32[]{:S(2)}) copy-start(f32[2048]{0:T(1024)S(1)} %get-tuple-element.84) | copy-start | bytes 24580
  156.9 23.4 %copy-start.10 = (bf16[1024,256]{0,1:T(8,128)(2,1)}, bf16[1024,256]{0,1:T(8,128)(2,1)S(1)}, u32[]{:S(2)}) copy-start(bf16[1024,256]{0,1:T(8,128)(2,1)S(1)} %slice.127) | copy-start | bytes 1572868
  171.0 9.3 copy-start.12
  184.4 0.8 copy-start.18
  210.1 6.8 copy-start.25
  214.9 1.0 copy-start
  214.9 42.1 %copy-start.31 = (f32[128]{0:T(128)}, f32[128]{0:T(128)S(1)}, u32[]{:S(2)}) copy-start(f32[128]{0:T(128)S(1)} %get-tuple-element.129) | copy-start | bytes 1540
  214.9 42.1 %copy-start.27 = (f32[128]{0:T(128)}, f32[128]{0:T(128)S(1)}, u32[]{:S(2)}) copy-start(f32[128]{0:T(128)S(1)} %fusion.86) | copy-start | bytes 1540
  216.9 542.5 %reduce-scatter.8.cloned.1.call-start = ((), (), s32[]{:S(2)}) async-start(), calls=%async_computation.12 | async-start | bytes 17301504 | tf_op jit(solution)/shard_map/reduce_scatter | solution.py:202
  432.7 15.8 %copy-start.5 = (bf16[2,32,32,2048]{3,2,1,0:T(8,128)(2,1)S(1)}, bf16[2,32,32,2048]{3,2,1,0:T(8,128)(2,1)}, u32[]{:S(2)}) copy-start(bf16[2,32,32,2048]{3,2,1,0:T(8,128)(2,1)} %copy.245) | copy-start | bytes 25165828
  463.5 19.9 %copy-start.34 = (bf16[2,2,1024,512]{3,2,1,0:T(8,128)(2,1)}, bf16[2,2,1024,512]{3,2,1,0:T(8,128)(2,1)S(1)}, u32[]{:S(2)}) copy-start(bf16[2,2,1024,512]{3,2,1,0:T(8,128)(2,1)S(1)} %get-tuple-element.133) | copy-start | bytes 12582916
  533.3 16.2 %copy-start.35 = (bf16[2,2,1024,512]{3,2,1,0:T(8,128)(2,1)}, bf16[2,2,1024,512]{3,2,1,0:T(8,128)(2,1)S(1)}, u32[]{:S(2)}) copy-start(bf16[2,2,1024,512]{3,2,1,0:T(8,128)(2,1)S(1)} %get-tuple-element.98) | copy-start | bytes 12582916
  577.2 1.0 copy-start.8
  577.2 16.3 %copy-start.26 = (s32[1,128,8]{1,2,0:T(8,128)S(1)}, s32[1,128,8]{1,2,0:T(8,128)}, u32[]{:S(2)}) copy-start(s32[1,128,8]{1,2,0:T(8,128)} %param.15) | copy-start | bytes 12292
  577.2 182.2 %copy-start.1 = (f32[128,2048]{1,0:T(8,128)S(1)}, f32[128,2048]{1,0:T(8,128)}, u32[]{:S(2)}) copy-start(f32[128,2048]{1,0:T(8,128)} %copy-done) | copy-start | bytes 3145732
  577.2 182.2 %copy-start.22 = (f32[2048]{0:T(1024)S(1)}, f32[2048]{0:T(1024)}, u32[]{:S(2)}) copy-start(f32[2048]{0:T(1024)} %copy-done.21) | copy-start | bytes 24580
  577.2 182.2 %copy-start.28 = (f32[128]{0:T(128)S(1)}, f32[128]{0:T(128)}, u32[]{:S(2)}) copy-start(f32[128]{0:T(128)} %copy-done.27) | copy-start | bytes 1540
  577.2 184.0 %copy-start.32 = (f32[128]{0:T(128)S(1)}, f32[128]{0:T(128)}, u32[]{:S(2)}) copy-start(f32[128]{0:T(128)} %copy-done.31) | copy-start | bytes 1540
  577.2 184.0 %copy-start.9 = (bf16[1,128,2048]{2,1,0:T(8,128)(2,1)S(1)}, bf16[1,128,2048]{2,1,0:T(8,128)(2,1)}, u32[]{:S(2)}) copy-start(bf16[1,128,2048]{2,1,0:T(8,128)(2,1)} %param.14) | copy-start | bytes 1572868
  579.6 13.9 %all-to-all-start.2 = ((f32[32,2,128]{2,1,0:T(2,128)}), f32[32,2,128]{2,1,0:T(2,128)S(1)}, u32[]{:S(2)}, u32[]{:S(2)}) async-start(f32[32,2,128]{2,1,0:T(2,128)} %get-tuple-element.92), calls=%async_computation.4 | async-start | bytes 65536 | tf_op jit(solution)/shard_map/all_to_all | solution.py:207
  582.5 254.3 %all-gather.13.cloned.1.call-start = ((), (), s32[]{:S(2)}) async-start(), calls=%async_computation.13 | async-start | bytes 4718592 | tf_op jit(solution)/shard_map/all_gather | solution.py:227
  762.4 162.2 %reduce-scatter.12.cloned.1.call-start = ((), (), s32[]{:S(2)}) async-start(), calls=%async_computation.15 | async-start | bytes 7864320 | tf_op jit(solution)/shard_map/reduce_scatter | solution.py:246
  762.6 84.0 %copy-start.11 = (bf16[1024,256]{0,1:T(8,128)(2,1)S(1)}, bf16[1024,256]{0,1:T(8,128)(2,1)}, u32[]{:S(2)}) copy-start(bf16[1024,256]{0,1:T(8,128)(2,1)} %copy-done.10) | copy-start | bytes 1572868
  836.7 9.9 slice-start
  840.8 5.9 slice-start.1
  846.7 1.4 copy-start.15
  846.7 1.4 copy-start.16
  846.7 3.4 copy-start.13
  846.7 3.4 copy-start.14
  848.1 3.4 copy-start.7
  848.1 3.4 copy-start.17
  850.1 6.5 copy-start.24
  850.2 6.5 copy-start.30
  863.7 3.5 copy-start.20
  867.1 179.5 %reduce-scatter.10.cloned.1.call-start = ((), (), s32[]{:S(2)}) async-start(), calls=%async_computation.14 | async-start | bytes 4718592 | tf_op jit(solution)/shard_map/reduce_scatter | solution.py:241
  875.1 357.9 %reduce-scatter.6.cloned.1.call-start = ((), (), s32[]{:S(2)}) async-start(), calls=%async_computation.11 | async-start | bytes 17301504 | tf_op jit(solution)/shard_map/reduce_scatter | solution.py:211
  886.3 1.2 copy-start.3
  886.3 382.2 %reduce-scatter.14.cloned.1.call-start = ((), (), s32[]{:S(2)}) async-start(), calls=%async_computation.16 | async-start | bytes 2621440 | tf_op jit(solution)/shard_map/reduce_scatter | solution.py:229
  887.7 16.9 %copy-start.19 = (bf16[2,128,1024]{2,1,0:T(8,128)(2,1)S(1)}, bf16[2,128,1024]{2,1,0:T(8,128)(2,1)}, u32[]{:S(2)}) copy-start(bf16[2,128,1024]{2,1,0:T(8,128)(2,1)} %copy-done.18) | copy-start | bytes 1572868
  887.7 16.9 %copy-start.33 = (bf16[1024,2048]{1,0:T(8,128)(2,1)S(1)}, bf16[1024,2048]{1,0:T(8,128)(2,1)}, u32[]{:S(2)}) copy-start(bf16[1024,2048]{1,0:T(8,128)(2,1)} %all-gather.13.cloned.1.call-done) | copy-start | bytes 12582916
  924.6 311.3 %all-to-all-start.3 = ((f32[8,64,768]{2,1,0:T(8,128)}), f32[8,64,768]{2,1,0:T(8,128)}, u32[]{:S(2)}, u32[]{:S(2)}) async-start(f32[8,64,768]{2,1,0:T(8,128)} %bitcast.266), calls=%async_computation.7 | async-start | bytes 3145728 | tf_op jit(solution)/shard_map/all_to_all | solution.py:247
Sparse Core Ops, SparseCore 0:
  44.9 30.1 all-gather.14
  78.0 100.6 all-gather.8
  181.6 118.1 all-gather.16
  302.5 112.5 all-gather.10
  577.4 181.9 reduce-scatter.7
  762.5 74.1 all-gather.12
  867.2 57.3 reduce-scatter.11
  928.2 118.2 reduce-scatter.9
  1048.9 184.1 reduce-scatter.5
  1236.0 32.5 reduce-scatter.13
